TPU v7x, 32 devices: a whole 2x2x4 slice. The times are simulated.
32 devices in a mesh: seq: 8 (over z, x), tp: 4 (over y, core).
Axes of the slice: x: 2, y: 2, z: 4, core: 2. Of those that a mesh axis runs over, the one named last changes fastest.
Arguments:
- inputs: bfloat16 [2, 2048, 2048], P(None, 'seq'), may hold values from -6 to 6
- cotangent: bfloat16 [2, 2048, 2048], P(None, 'seq'), may hold values from -6 to 6
- attn_gain: bfloat16 [2048], P('seq'), may hold values from 0.5 to 1.5
- w_query: bfloat16 [2048, 2048], P('seq', 'tp'), may hold values from -0.125 to 0.125
- w_key: bfloat16 [2048, 2048], P('seq', 'tp'), may hold values from -0.125 to 0.125
- w_value: bfloat16 [2048, 3456], P('seq', 'tp'), may hold values from -0.125 to 0.125
- w_gate: bfloat16 [2048, 3456], P('seq', 'tp'), may hold values from -0.125 to 0.125
- w_out: bfloat16 [3456, 2048], P('tp', 'seq'), may hold values from -0.15625 to 0.15625
- ffn_gain: bfloat16 [2048], P('seq'), may hold values from 0.5 to 1.5
- w_glu: bfloat16 [2048, 3456], P('seq', 'tp'), may hold values from -0.125 to 0.125
- w_up: bfloat16 [2048, 3456], P('seq', 'tp'), may hold values from -0.125 to 0.125
- w_down: bfloat16 [3456, 2048], P('tp', 'seq'), may hold values from -0.15625 to 0.15625
- decay_rate: float32 [8], P('tp'), may hold values from 0 to 0.032, as said below
Outputs:
- outputs: bfloat16 [2, 2048, 2048], P(None, 'seq')
- input_grad: float32 [2, 2048, 2048], P(None, 'seq')
- attngain_grad: float32 [2048], P('seq')
- query_grad: float32 [2048, 2048], P('seq', 'tp')
- key_grad: float32 [2048, 2048], P('seq', 'tp')
- value_grad: float32 [2048, 3456], P('seq', 'tp')
- gate_grad: float32 [2048, 3456], P('seq', 'tp')
- out_grad: float32 [3456, 2048], P('tp', 'seq')
- ffngain_grad: float32 [2048], P('seq')
- glu_grad: float32 [2048, 3456], P('seq', 'tp')
- up_grad: float32 [2048, 3456], P('seq', 'tp')
- down_grad: float32 [3456, 2048], P('tp', 'seq')
Inputs may be any that keep to these rules, and one draw needn't show every extreme that they name: `decay_rate`: each head's decay rate; positive.
All inputs are finite; a program needn't handle non-finite values.
Results may differ from a plain program's by a relative error of at most 0.03.
Values may be sent and summed in bfloat16 or wider, within the bound.
A program may use at most 256 MiB of HBM per device.

v0:
```python
import math
import jax
import jax.numpy as jnp
from jax import lax
from jax.sharding import PartitionSpec as P

KEY = 256
VAL = 432
EPS_LAYER = 1e-05
EPS_GROUP = 1e-06
MAXIMAL_ACCURACY = lax.Precision.HIGHEST


def passed_along(block, axis, distance):
    devices = range(lax.axis_size(axis))
    route = [(i - distance, i) for i in devices if i - distance in devices]
    return lax.ppermute(block, axis, route)


def normalize(values, epsilon):
    average = jnp.mean(values, axis=-1, keepdims=True)
    centred = values - average
    inv_std = lax.rsqrt(jnp.mean(centred * centred, axis=-1, keepdims=True) + epsilon)
    return (centred * inv_std, inv_std)


def normalize_back(upstream, normed, inv_std):
    return inv_std * (
        upstream
        - jnp.mean(upstream, axis=-1, keepdims=True)
        - normed * jnp.mean(upstream * normed, axis=-1, keepdims=True)
    )


def swish_parts(values):
    sigmoid = jax.nn.sigmoid(values)
    return (values * sigmoid, sigmoid * (1.0 + values * (1.0 - sigmoid)))


def rotary_tables(positions, width):
    half_width = width // 2
    fraction = jnp.arange(half_width, dtype=jnp.float32) / max(half_width - 1, 1)
    frequency = jnp.power(10000.0, -fraction)
    angles = positions[:, None] * frequency[None, :]
    cosine = jnp.concatenate([jnp.cos(angles), jnp.cos(angles)], axis=-1)[:, None, :]
    sine_table = jnp.concatenate([jnp.sin(angles), jnp.sin(angles)], axis=-1)[:, None, :]
    return (cosine, sine_table)


def rotate(values, cosine, sine_table):
    half_width = values.shape[-1] // 2
    turned = jnp.concatenate([-values[..., half_width:], values[..., :half_width]], axis=-1)
    return values * cosine + turned * sine_table


def rotate_back(upstream, cosine, sine_table):
    half_width = upstream.shape[-1] // 2
    scaled = upstream * sine_table
    turned = jnp.concatenate([scaled[..., half_width:], -scaled[..., :half_width]], axis=-1)
    return upstream * cosine + turned


def decay_tables(rates, length):
    offsets = jnp.arange(length, dtype=jnp.float32)
    distance = offsets[:, None] - offsets[None, :]
    decay_mask = jnp.where(
        distance[None] >= 0.0,
        jnp.exp(-rates[:, None, None] * jnp.maximum(distance, 0.0)[None]),
        0.0,
    )
    leading_decay = jnp.exp(-rates[None, :] * (offsets[:, None] + 1.0))
    trailing_decay = jnp.exp(-rates[None, :] * (length - 1.0 - offsets[:, None]))
    return (decay_mask, leading_decay, trailing_decay)


def block_summary(key_rotated, value_matrix_rows, trailing_decay):
    return jnp.einsum(
        "ysu,ysb->sub",
        key_rotated.astype(jnp.float32) * trailing_decay[:, :, None],
        value_matrix_rows.astype(jnp.float32),
        precision=MAXIMAL_ACCURACY,
    )


def block_weights(query_rotated, key_rotated, decay_mask):
    scores = jnp.einsum(
        "ihk,jhk->hij", query_rotated, key_rotated, preferred_element_type=jnp.float32
    )
    return (scores * decay_mask).astype(jnp.bfloat16)


def block_output(
    query_rotated, key_rotated, value_matrix_rows, incoming_state, decay_mask, leading_decay
):
    layer_weights = block_weights(query_rotated, key_rotated, decay_mask)
    inner = jnp.einsum(
        "hij,jhv->ihv", layer_weights, value_matrix_rows, preferred_element_type=jnp.float32
    )
    carried_state = jnp.einsum(
        "jnq,nqs->jns",
        query_rotated.astype(jnp.float32) * leading_decay[:, :, None],
        incoming_state,
        precision=MAXIMAL_ACCURACY,
    )
    return inner + carried_state


def state_grad_own(query_rotated, output_gradient, leading_decay):
    return jnp.einsum(
        "pxa,pxb->xab",
        query_rotated.astype(jnp.float32) * leading_decay[:, :, None],
        output_gradient.astype(jnp.float32),
        precision=MAXIMAL_ACCURACY,
    )


def block_backward(
    query_rotated,
    key_rotated,
    value_matrix_rows,
    incoming_state,
    state_gradient,
    output_gradient,
    decay_mask,
    leading_decay,
    trailing_decay,
):
    weight_gradients = (
        jnp.einsum(
            "ihv,jhv->hij", output_gradient, value_matrix_rows, preferred_element_type=jnp.float32
        )
        * decay_mask
    ).astype(jnp.bfloat16)
    layer_weights = block_weights(query_rotated, key_rotated, decay_mask)
    query_gradient = jnp.einsum(
        "pzg,gpe->zpe", weight_gradients, key_rotated, preferred_element_type=jnp.float32
    ) + leading_decay[:, :, None] * jnp.einsum(
        "wcr,cdr->wcd",
        output_gradient.astype(jnp.float32),
        incoming_state,
        precision=MAXIMAL_ACCURACY,
    )
    key_gradient = jnp.einsum(
        "zun,uzf->nzf", weight_gradients, query_rotated, preferred_element_type=jnp.float32
    ) + trailing_decay[:, :, None] * jnp.einsum(
        "crp,rnp->crn",
        value_matrix_rows.astype(jnp.float32),
        state_gradient,
        precision=MAXIMAL_ACCURACY,
    )
    value_gradient = jnp.einsum(
        "lpb,plz->blz", layer_weights, output_gradient, preferred_element_type=jnp.float32
    ) + trailing_decay[:, :, None] * jnp.einsum(
        "zmf,mfn->zmn", key_rotated.astype(jnp.float32), state_gradient, precision=MAXIMAL_ACCURACY
    )
    return (query_gradient, key_gradient, value_gradient)


def carry_states(whole_decay, summary):

    def advance(turn_index, carried_state):
        return passed_along(whole_decay * carried_state + summary, "seq", 1)

    return lax.fori_loop(0, lax.axis_size("seq") - 1, advance, jnp.zeros_like(summary))


def carry_back(whole_decay, own_grad):

    def retreat(turn_index, carried_state):
        return passed_along(whole_decay * carried_state + own_grad, "seq", -1)

    return lax.fori_loop(0, lax.axis_size("seq") - 1, retreat, jnp.zeros_like(own_grad))


def on_device(
    inputs,
    cotangent,
    attn_gain,
    w_query,
    w_key,
    w_value,
    w_gate,
    w_out,
    ffn_gain,
    w_glu,
    w_up,
    w_down,
    decay_rate,
):
    seq_count, tok_rows, model_width = inputs.shape
    row_count = seq_count * tok_rows
    local_heads = decay_rate.shape[0]
    gathered = (
        lax.all_gather(w_query, "seq", axis=0, tiled=True),
        lax.all_gather(w_key, "seq", axis=0, tiled=True),
        lax.all_gather(w_value, "seq", axis=0, tiled=True),
        lax.all_gather(w_gate, "seq", axis=0, tiled=True),
        lax.all_gather(w_out, "seq", axis=1, tiled=True),
        lax.all_gather(w_glu, "seq", axis=0, tiled=True),
        lax.all_gather(w_up, "seq", axis=0, tiled=True),
        lax.all_gather(w_down, "seq", axis=1, tiled=True),
        lax.all_gather(attn_gain, "seq", axis=0, tiled=True),
        lax.all_gather(ffn_gain, "seq", axis=0, tiled=True),
    )
    (
        full_query,
        full_key,
        full_value,
        full_gate,
        full_out,
        full_glu,
        full_up,
        full_down,
        full_attn_gain,
        full_ffn_gain,
    ) = gathered
    residual = inputs.astype(jnp.float32).reshape(row_count, model_width)
    normed_one, inv_one = normalize(residual, EPS_LAYER)
    attn_in = (normed_one * full_attn_gain.astype(jnp.float32)).astype(jnp.bfloat16)
    query_lin = jnp.dot(attn_in, full_query, preferred_element_type=jnp.float32)
    key_lin = jnp.dot(attn_in, full_key, preferred_element_type=jnp.float32)
    value_lin = jnp.dot(attn_in, full_value, preferred_element_type=jnp.float32)
    gate_lin = jnp.dot(attn_in, full_gate, preferred_element_type=jnp.float32)
    offset = (lax.axis_index("seq") * tok_rows).astype(jnp.float32)
    positions = offset + jnp.arange(tok_rows, dtype=jnp.float32)
    cosine, sine_table = rotary_tables(positions, KEY)
    key_scale = 1.0 / math.sqrt(KEY)
    query_rotated = rotate(
        query_lin.reshape(seq_count, tok_rows, local_heads, KEY), cosine, sine_table
    ).astype(jnp.bfloat16)
    key_rotated = (
        rotate(key_lin.reshape(seq_count, tok_rows, local_heads, KEY), cosine, sine_table)
        * key_scale
    ).astype(jnp.bfloat16)
    value_matrix_rows = value_lin.reshape(seq_count, tok_rows, local_heads, VAL).astype(
        jnp.bfloat16
    )
    decay_mask, leading_decay, trailing_decay = decay_tables(decay_rate, tok_rows)
    whole_decay = jnp.exp(-decay_rate * tok_rows)[:, None, None]
    summary = jax.vmap(block_summary, in_axes=(0, 0, None))(
        key_rotated, value_matrix_rows, trailing_decay
    )
    incoming_state = carry_states(whole_decay, summary)
    retained = jax.vmap(block_output, in_axes=(0, 0, 0, 0, None, None))(
        query_rotated, key_rotated, value_matrix_rows, incoming_state, decay_mask, leading_decay
    )
    group_normed, group_inv = normalize(retained, EPS_GROUP)
    gate_act, gate_slope = swish_parts(gate_lin)
    group_flat = group_normed.reshape(row_count, local_heads * VAL)
    mixed = (gate_act * group_flat).astype(jnp.bfloat16)
    attn_out = lax.psum(jnp.dot(mixed, full_out, preferred_element_type=jnp.float32), "tp")
    middle = residual + attn_out
    normed_two, inv_two = normalize(middle, EPS_LAYER)
    ffn_in = (normed_two * full_ffn_gain.astype(jnp.float32)).astype(jnp.bfloat16)
    glu_lin = jnp.dot(ffn_in, full_glu, preferred_element_type=jnp.float32)
    up_lin = jnp.dot(ffn_in, full_up, preferred_element_type=jnp.float32)
    glu_act, glu_slope = swish_parts(glu_lin)
    hidden = (glu_act * up_lin).astype(jnp.bfloat16)
    ffn_out = lax.psum(jnp.dot(hidden, full_down, preferred_element_type=jnp.float32), "tp")
    final = middle + ffn_out
    outputs = final.astype(jnp.bfloat16).reshape(seq_count, tok_rows, model_width)
    back_weights = (
        lax.all_gather(w_query, "seq", axis=0, tiled=True),
        lax.all_gather(w_key, "seq", axis=0, tiled=True),
        lax.all_gather(w_value, "seq", axis=0, tiled=True),
        lax.all_gather(w_gate, "seq", axis=0, tiled=True),
        lax.all_gather(w_out, "seq", axis=1, tiled=True),
        lax.all_gather(w_glu, "seq", axis=0, tiled=True),
        lax.all_gather(w_up, "seq", axis=0, tiled=True),
        lax.all_gather(w_down, "seq", axis=1, tiled=True),
        lax.all_gather(attn_gain, "seq", axis=0, tiled=True),
        lax.all_gather(ffn_gain, "seq", axis=0, tiled=True),
    )
    (
        back_query,
        back_key,
        back_value,
        back_gate,
        back_out,
        back_glu,
        back_up,
        back_down,
        back_attn_gain,
        back_ffn_gain,
    ) = back_weights
    cot_rows = cotangent.reshape(row_count, model_width)
    down_grad = jnp.dot(hidden.T, cot_rows, preferred_element_type=jnp.float32)
    grad_hidden = jnp.dot(cot_rows, back_down.T, preferred_element_type=jnp.float32)
    grad_glu = (grad_hidden * up_lin * glu_slope).astype(jnp.bfloat16)
    grad_up = (grad_hidden * glu_act).astype(jnp.bfloat16)
    glu_grad = jnp.dot(ffn_in.T, grad_glu, preferred_element_type=jnp.float32)
    up_grad = jnp.dot(ffn_in.T, grad_up, preferred_element_type=jnp.float32)
    grad_ffn_in = lax.psum(
        jnp.dot(grad_glu, back_glu.T, preferred_element_type=jnp.float32)
        + jnp.dot(grad_up, back_up.T, preferred_element_type=jnp.float32),
        "tp",
    )
    ffngain_grad = jnp.sum(grad_ffn_in * normed_two, axis=0)
    grad_middle = cot_rows.astype(jnp.float32) + normalize_back(
        grad_ffn_in * back_ffn_gain.astype(jnp.float32), normed_two, inv_two
    )
    grad_middle_bf = grad_middle.astype(jnp.bfloat16)
    out_grad = jnp.dot(mixed.T, grad_middle_bf, preferred_element_type=jnp.float32)
    grad_mixed = jnp.dot(grad_middle_bf, back_out.T, preferred_element_type=jnp.float32)
    grad_gate = (grad_mixed * group_flat * gate_slope).astype(jnp.bfloat16)
    grad_group = (grad_mixed * gate_act).reshape(seq_count, tok_rows, local_heads, VAL)
    grad_retained = normalize_back(grad_group, group_normed, group_inv).astype(jnp.bfloat16)
    own_grad = jax.vmap(state_grad_own, in_axes=(0, 0, None))(
        query_rotated, grad_retained, leading_decay
    )
    state_gradient = carry_back(whole_decay, own_grad)
    grad_qrot, grad_krot, grad_vrows = jax.vmap(
        block_backward, in_axes=(0, 0, 0, 0, 0, 0, None, None, None)
    )(
        query_rotated,
        key_rotated,
        value_matrix_rows,
        incoming_state,
        state_gradient,
        grad_retained,
        decay_mask,
        leading_decay,
        trailing_decay,
    )
    query_gradient = (
        rotate_back(grad_qrot, cosine, sine_table)
        .reshape(row_count, local_heads * KEY)
        .astype(jnp.bfloat16)
    )
    key_gradient = (
        (rotate_back(grad_krot, cosine, sine_table) * key_scale)
        .reshape(row_count, local_heads * KEY)
        .astype(jnp.bfloat16)
    )
    value_gradient = grad_vrows.reshape(row_count, local_heads * VAL).astype(jnp.bfloat16)
    query_grad = jnp.dot(attn_in.T, query_gradient, preferred_element_type=jnp.float32)
    key_grad = jnp.dot(attn_in.T, key_gradient, preferred_element_type=jnp.float32)
    value_grad = jnp.dot(attn_in.T, value_gradient, preferred_element_type=jnp.float32)
    gate_grad = jnp.dot(attn_in.T, grad_gate, preferred_element_type=jnp.float32)
    partial_in = (
        jnp.dot(query_gradient, back_query.T, preferred_element_type=jnp.float32)
        + jnp.dot(key_gradient, back_key.T, preferred_element_type=jnp.float32)
        + jnp.dot(value_gradient, back_value.T, preferred_element_type=jnp.float32)
        + jnp.dot(grad_gate, back_gate.T, preferred_element_type=jnp.float32)
    )
    grad_attn_in = lax.psum(partial_in, "tp")
    attngain_grad = jnp.sum(grad_attn_in * normed_one, axis=0)
    input_grad = grad_middle + normalize_back(
        grad_attn_in * back_attn_gain.astype(jnp.float32), normed_one, inv_one
    )
    input_out = input_grad.reshape(seq_count, tok_rows, model_width)
    reduced = (
        lax.psum_scatter(query_grad, "seq", scatter_dimension=0, tiled=True),
        lax.psum_scatter(key_grad, "seq", scatter_dimension=0, tiled=True),
        lax.psum_scatter(value_grad, "seq", scatter_dimension=0, tiled=True),
        lax.psum_scatter(gate_grad, "seq", scatter_dimension=0, tiled=True),
        lax.psum_scatter(out_grad, "seq", scatter_dimension=1, tiled=True),
        lax.psum_scatter(glu_grad, "seq", scatter_dimension=0, tiled=True),
        lax.psum_scatter(up_grad, "seq", scatter_dimension=0, tiled=True),
        lax.psum_scatter(down_grad, "seq", scatter_dimension=1, tiled=True),
        lax.psum_scatter(attngain_grad, "seq", scatter_dimension=0, tiled=True),
        lax.psum_scatter(ffngain_grad, "seq", scatter_dimension=0, tiled=True),
    )
    return (
        outputs,
        input_out,
        reduced[8],
        reduced[0],
        reduced[1],
        reduced[2],
        reduced[3],
        reduced[4],
        reduced[9],
        reduced[5],
        reduced[6],
        reduced[7],
    )


def solution(mesh):
    return jax.shard_map(
        on_device,
        mesh=mesh,
        in_specs=(
            P(None, "seq", None),
            P(None, "seq", None),
            P("seq"),
            P("seq", "tp"),
            P("seq", "tp"),
            P("seq", "tp"),
            P("seq", "tp"),
            P("tp", "seq"),
            P("seq"),
            P("seq", "tp"),
            P("seq", "tp"),
            P("tp", "seq"),
            P("tp"),
        ),
        out_specs=(
            P(None, "seq", None),
            P(None, "seq", None),
            P("seq"),
            P("seq", "tp"),
            P("seq", "tp"),
            P("seq", "tp"),
            P("seq", "tp"),
            P("tp", "seq"),
            P("seq"),
            P("seq", "tp"),
            P("seq", "tp"),
            P("tp", "seq"),
        ),
        check_vma=False,
    )
```

profile of v0, /device:TPU:0, one launch (start us, length us, event | category | flops | bytes accessed | tf_op | source)
XLA Modules:
  0.0 2463.8 jit_solution(17136700813776060130)
XLA Ops:
  66.0 45.9 %all-gather.15.cloned.1.call-done = bf16[2048,512]{1,0:T(8,128)(2,1)} async-done(((bf16[256,512]{1,0:T(8,128)(2,1)}), bf16[2048,512]{1,0:T(8,128)(2,1)}) %all-gather.15.cloned.1.call-update) | async-done | bytes 2097168 | tf_op jit(solution)/shard_map/all_gather | solution.py:194
  122.3 57.4 %all-gather.13.cloned.1.call-done = bf16[2048,864]{0,1:T(8,128)(2,1)} async-done(((bf16[256,864]{0,1:T(8,128)(2,1)}), bf16[2048,864]{0,1:T(8,128)(2,1)}) %all-gather.13.cloned.1.call-update) | async-done | bytes 3538960 | tf_op jit(solution)/shard_map/all_gather | solution.py:196
  186.6 373.1 %while.20 = (s32[]{:T(128)}, f32[2,2,256,432]{2,3,1,0:T(8,128)S(1)}, f32[2]{0:T(128)S(1)}, f32[2,2,256,432]{2,3,1,0:T(8,128)S(1)}, s32[]{:T(128)}) while((s32[]{:T(128)}, f32[2,2,256,432]{2,3,1,0:T(8,128)S(1)}, f32[2]{0:T(128)S(1)}, f32[2,2,256,432]{2,3,1,0:T(8,128)S(1)}, s32[]{:T(128)}) %tuple.65), condition=%wide.region_3.4_spmd, body=%wide.region_2.3_spmd.sunk | while | flops 884738 | bytes 12386413 | solution.py:164
  191.6 48.9 %collective-permute-done = f32[2,2,256,432]{2,3,1,0:T(8,128)S(1)} collective-permute-done((f32[2,2,256,432]{2,3,1,0:T(8,128)}, f32[2,2,256,432]{2,3,1,0:T(8,128)S(1)}, u32[]{:S(2)}, u32[]{:S(2)}) %collective-permute-start) | collective-permute-done | bytes 1769504 | tf_op jit(solution)/shard_map/while/body/eval_jaxpr/ppermute | solution.py:17
  265.2 42.4 %collective-permute-done = f32[2,2,256,432]{2,3,1,0:T(8,128)S(1)} collective-permute-done((f32[2,2,256,432]{2,3,1,0:T(8,128)}, f32[2,2,256,432]{2,3,1,0:T(8,128)S(1)}, u32[]{:S(2)}, u32[]{:S(2)}) %collective-permute-start) | collective-permute-done | bytes 1769504 | tf_op jit(solution)/shard_map/while/body/eval_jaxpr/ppermute | solution.py:17
  327.7 50.1 %collective-permute-done = f32[2,2,256,432]{2,3,1,0:T(8,128)S(1)} collective-permute-done((f32[2,2,256,432]{2,3,1,0:T(8,128)}, f32[2,2,256,432]{2,3,1,0:T(8,128)S(1)}, u32[]{:S(2)}, u32[]{:S(2)}) %collective-permute-start) | collective-permute-done | bytes 1769504 | tf_op jit(solution)/shard_map/while/body/eval_jaxpr/ppermute | solution.py:17
  601.9 65.3 %all-reduce.8.cloned.1.call-done = f32[512,2048]{1,0:T(8,128)} async-done(((f32[512,2048]{1,0:T(8,128)}), f32[512,2048]{1,0:T(8,128)}) %all-reduce.8.cloned.1.call-update) | async-done | bytes 4194320 | tf_op jit(solution)/shard_map/psum | solution.py:251
  674.6 62.0 %all-gather.21.cloned.1.call-done = bf16[2048,864]{0,1:T(8,128)(2,1)} async-done(((bf16[256,864]{0,1:T(8,128)(2,1)}), bf16[2048,864]{0,1:T(8,128)(2,1)}) %all-gather.21.cloned.1.call-update) | async-done | bytes 3538960 | tf_op jit(solution)/shard_map/all_gather | solution.py:199
  742.5 61.6 %all-gather.23.cloned.1.call-done = bf16[2048,864]{0,1:T(8,128)(2,1)} async-done(((bf16[256,864]{0,1:T(8,128)(2,1)}), bf16[2048,864]{0,1:T(8,128)(2,1)}) %all-gather.23.cloned.1.call-update) | async-done | bytes 3538960 | tf_op jit(solution)/shard_map/all_gather | solution.py:200
  809.9 61.5 %all-gather.25.cloned.1.call-done = bf16[864,2048]{1,0:T(8,128)(2,1)} async-done(((bf16[864,256]{1,0:T(8,128)(2,1)}), bf16[864,2048]{1,0:T(8,128)(2,1)}) %all-gather.25.cloned.1.call-update) | async-done | bytes 3538960 | tf_op jit(solution)/shard_map/all_gather | solution.py:201
  893.1 76.8 %all-reduce.10.cloned.1.call-done = f32[512,2048]{1,0:T(8,128)} async-done(((f32[512,2048]{1,0:T(8,128)}), f32[512,2048]{1,0:T(8,128)}) %all-reduce.10.cloned.1.call-update) | async-done | bytes 4194320 | tf_op jit(solution)/shard_map/psum | solution.py:293
  1001.3 293.0 %while.21 = (s32[]{:T(128)}, f32[2,2,256,432]{2,3,1,0:T(8,128)S(1)}, f32[2]{0:T(128)S(1)}, f32[2,2,256,432]{2,3,1,0:T(8,128)S(1)}, s32[]{:T(128)}) while((s32[]{:T(128)}, f32[2,2,256,432]{2,3,1,0:T(8,128)S(1)}, f32[2]{0:T(128)S(1)}, f32[2,2,256,432]{2,3,1,0:T(8,128)S(1)}, s32[]{:T(128)}) %tuple.110), condition=%wide.region_16.17_spmd, body=%wide.region_15.16_spmd.sunk | while | flops 884738 | bytes 12386413 | solution.py:172
  1004.1 40.8 %collective-permute-done.1 = f32[2,2,256,432]{2,3,1,0:T(8,128)S(1)} collective-permute-done((f32[2,2,256,432]{2,3,1,0:T(8,128)}, f32[2,2,256,432]{2,3,1,0:T(8,128)S(1)}, u32[]{:S(2)}, u32[]{:S(2)}) %collective-permute-start.1) | collective-permute-done | bytes 1769504 | tf_op jit(solution)/shard_map/while/body/eval_jaxpr/ppermute | solution.py:17
  1047.8 40.6 %collective-permute-done.1 = f32[2,2,256,432]{2,3,1,0:T(8,128)S(1)} collective-permute-done((f32[2,2,256,432]{2,3,1,0:T(8,128)}, f32[2,2,256,432]{2,3,1,0:T(8,128)S(1)}, u32[]{:S(2)}, u32[]{:S(2)}) %collective-permute-start.1) | collective-permute-done | bytes 1769504 | tf_op jit(solution)/shard_map/while/body/eval_jaxpr/ppermute | solution.py:17
  1091.2 40.0 %collective-permute-done.1 = f32[2,2,256,432]{2,3,1,0:T(8,128)S(1)} collective-permute-done((f32[2,2,256,432]{2,3,1,0:T(8,128)}, f32[2,2,256,432]{2,3,1,0:T(8,128)S(1)}, u32[]{:S(2)}, u32[]{:S(2)}) %collective-permute-start.1) | collective-permute-done | bytes 1769504 | tf_op jit(solution)/shard_map/while/body/eval_jaxpr/ppermute | solution.py:17
  1373.0 101.1 %all-reduce.12.cloned.1.call-done = (f32[512,2048]{1,0:T(8,128)}, f32[512,2048]{1,0:T(8,128)}) async-done(((f32[512,2048]{1,0:T(8,128)}, f32[512,2048]{1,0:T(8,128)}), (f32[512,2048]{1,0:T(8,128)}, f32[512,2048]{1,0:T(8,128)})) %all-reduce.12.cloned.1.call-update) | async-done | bytes 8388624 | tf_op jit(solution)/shard_map/psum | solution.py:259
  1527.2 39.8 %reduce-scatter.11.cloned.1.call-done = f32[256,512]{1,0:T(8,128)} async-done(((f32[2048,512]{1,0:T(8,128)}), f32[256,512]{1,0:T(8,128)}) %reduce-scatter.11.cloned.1.call-update) | async-done | bytes 524304 | tf_op jit(solution)/shard_map/reduce_scatter | solution.py:354
  1567.0 92.2 %reduce-scatter.9.cloned.1.call-done = f32[256,512]{1,0:T(8,128)} async-done(((f32[2048,512]{1,0:T(8,128)}), f32[256,512]{1,0:T(8,128)}) %reduce-scatter.9.cloned.1.call-update) | async-done | bytes 524304 | tf_op jit(solution)/shard_map/reduce_scatter | solution.py:353
  1659.2 133.3 %reduce-scatter.19.cloned.1.call-done = f32[256,864]{0,1:T(8,128)} async-done(((f32[2048,864]{0,1:T(8,128)}), f32[256,864]{0,1:T(8,128)}) %reduce-scatter.19.cloned.1.call-update) | async-done | bytes 884752 | tf_op jit(solution)/shard_map/reduce_scatter | solution.py:358
  1792.5 132.8 %reduce-scatter.21.cloned.1.call-done = f32[256,864]{0,1:T(8,128)} async-done(((f32[2048,864]{0,1:T(8,128)}), f32[256,864]{0,1:T(8,128)}) %reduce-scatter.21.cloned.1.call-update) | async-done | bytes 884752 | tf_op jit(solution)/shard_map/reduce_scatter | solution.py:359
  1925.3 132.8 %reduce-scatter.23.cloned.1.call-done = f32[864,256]{1,0:T(8,128)} async-done(((f32[864,2048]{1,0:T(8,128)}), f32[864,256]{1,0:T(8,128)}) %reduce-scatter.23.cloned.1.call-update) | async-done | bytes 884752 | tf_op jit(solution)/shard_map/reduce_scatter | solution.py:360
  2058.2 132.8 %reduce-scatter.17.cloned.1.call-done = f32[864,256]{1,0:T(8,128)} async-done(((f32[864,2048]{1,0:T(8,128)}), f32[864,256]{1,0:T(8,128)}) %reduce-scatter.17.cloned.1.call-update) | async-done | bytes 884752 | tf_op jit(solution)/shard_map/reduce_scatter | solution.py:357
  2191.0 132.8 %reduce-scatter.13.cloned.1.call-done = f32[256,864]{0,1:T(8,128)} async-done(((f32[2048,864]{0,1:T(8,128)}), f32[256,864]{0,1:T(8,128)}) %reduce-scatter.13.cloned.1.call-update) | async-done | bytes 884752 | tf_op jit(solution)/shard_map/reduce_scatter | solution.py:355
  2323.8 133.0 %reduce-scatter.15.cloned.1.call-done = f32[256,864]{0,1:T(8,128)} async-done(((f32[2048,864]{0,1:T(8,128)}), f32[256,864]{0,1:T(8,128)}) %reduce-scatter.15.cloned.1.call-update) | async-done | bytes 884752 | tf_op jit(solution)/shard_map/reduce_scatter | solution.py:356
  (319 shorter events, 722.8 us)
Async XLA Ops:
  7.2 54.9 %all-gather.17.cloned.1.call-start = ((), (), s32[]{:S(2)}) async-start(), calls=%async_computation.11 | async-start | bytes 2359296 | tf_op jit(solution)/shard_map/all_gather | solution.py:195
  7.9 103.9 %all-gather.15.cloned.1.call-start = ((), (), s32[]{:S(2)}) async-start(), calls=%async_computation.10 | async-start | bytes 2359296 | tf_op jit(solution)/shard_map/all_gather | solution.py:194
  8.7 171.0 %all-gather.13.cloned.1.call-start = ((), (), s32[]{:S(2)}) async-start(), calls=%async_computation.9 | async-start | bytes 3981312 | tf_op jit(solution)/shard_map/all_gather | solution.py:196
  9.4 556.9 %all-gather.11.cloned.1.call-start = ((), (), s32[]{:S(2)}) async-start(), calls=%async_computation.8 | async-start | bytes 3981312 | tf_op jit(solution)/shard_map/all_gather | solution.py:197
  10.0 563.2 %all-gather.19.cloned.1.call-start = ((), (), s32[]{:S(2)}) async-start(), calls=%async_computation.12 | async-start | bytes 3981312 | tf_op jit(solution)/shard_map/all_gather | solution.py:198
  10.6 656.7 %all-reduce.8.cloned.1.call-start = ((), (), s32[]{:S(2)}) async-start(), calls=%async_computation.13 | async-start | bytes 8388608 | tf_op jit(solution)/shard_map/psum | solution.py:251
  188.2 52.4 %collective-permute-start = (f32[2,2,256,432]{2,3,1,0:T(8,128)}, f32[2,2,256,432]{2,3,1,0:T(8,128)S(1)}, u32[]{:S(2)}, u32[]{:S(2)}) collective-permute-start(f32[2,2,256,432]{2,3,1,0:T(8,128)} %multiply_add_fusion.5), channel_id=1, source_target_pairs={{0,4},{4,8},{8,12},{12,16},{16,20},{20,24},{24,28},{1,5},{5,9},{9,... | collective-permute-start | bytes 5308424 | tf_op jit(solution)/shard_map/while/body/eval_jaxpr/ppermute | solution.py:17
  242.2 65.5 %collective-permute-start = (f32[2,2,256,432]{2,3,1,0:T(8,128)}, f32[2,2,256,432]{2,3,1,0:T(8,128)S(1)}, u32[]{:S(2)}, u32[]{:S(2)}) collective-permute-start(f32[2,2,256,432]{2,3,1,0:T(8,128)} %multiply_add_fusion.5), channel_id=1, source_target_pairs={{0,4},{4,8},{8,12},{12,16},{16,20},{20,24},{24,28},{1,5},{5,9},{9,... | collective-permute-start | bytes 5308424 | tf_op jit(solution)/shard_map/while/body/eval_jaxpr/ppermute | solution.py:17
  309.3 68.5 %collective-permute-start = (f32[2,2,256,432]{2,3,1,0:T(8,128)}, f32[2,2,256,432]{2,3,1,0:T(8,128)S(1)}, u32[]{:S(2)}, u32[]{:S(2)}) collective-permute-start(f32[2,2,256,432]{2,3,1,0:T(8,128)} %multiply_add_fusion.5), channel_id=1, source_target_pairs={{0,4},{4,8},{8,12},{12,16},{16,20},{20,24},{24,28},{1,5},{5,9},{9,... | collective-permute-start | bytes 5308424 | tf_op jit(solution)/shard_map/while/body/eval_jaxpr/ppermute | solution.py:17
  379.3 51.4 %collective-permute-start = (f32[2,2,256,432]{2,3,1,0:T(8,128)}, f32[2,2,256,432]{2,3,1,0:T(8,128)S(1)}, u32[]{:S(2)}, u32[]{:S(2)}) collective-permute-start(f32[2,2,256,432]{2,3,1,0:T(8,128)} %multiply_add_fusion.5), channel_id=1, source_target_pairs={{0,4},{4,8},{8,12},{12,16},{16,20},{20,24},{24,28},{1,5},{5,9},{9,... | collective-permute-start | bytes 5308424 | tf_op jit(solution)/shard_map/while/body/eval_jaxpr/ppermute | solution.py:17
  579.9 156.7 %all-gather.21.cloned.1.call-start = ((), (), s32[]{:S(2)}) async-start(), calls=%async_computation.14 | async-start | bytes 3981312 | tf_op jit(solution)/shard_map/all_gather | solution.py:199
  580.6 223.4 %all-gather.23.cloned.1.call-start = ((), (), s32[]{:S(2)}) async-start(), calls=%async_computation.15 | async-start | bytes 3981312 | tf_op jit(solution)/shard_map/all_gather | solution.py:200
  581.4 290.1 %all-gather.25.cloned.1.call-start = ((), (), s32[]{:S(2)}) async-start(), calls=%async_computation.16 | async-start | bytes 3981312 | tf_op jit(solution)/shard_map/all_gather | solution.py:201
  582.1 387.7 %all-reduce.10.cloned.1.call-start = ((), (), s32[]{:S(2)}) async-start(), calls=%async_computation.17 | async-start | bytes 8388608 | tf_op jit(solution)/shard_map/psum | solution.py:293
  886.0 588.0 %all-reduce.12.cloned.1.call-start = ((), (), s32[]{:S(2)}) async-start(), calls=%async_computation.26 | async-start | bytes 16777216 | tf_op jit(solution)/shard_map/psum | solution.py:259
  1002.8 42.1 %collective-permute-start.1 = (f32[2,2,256,432]{2,3,1,0:T(8,128)}, f32[2,2,256,432]{2,3,1,0:T(8,128)S(1)}, u32[]{:S(2)}, u32[]{:S(2)}) collective-permute-start(f32[2,2,256,432]{2,3,1,0:T(8,128)} %multiply_add_fusion.6), channel_id=1, source_target_pairs={{4,0},{8,4},{12,8},{16,12},{20,16},{24,20},{28,24},{5,1},{9,5},{13... | collective-permute-start | bytes 5308424 | tf_op jit(solution)/shard_map/while/body/eval_jaxpr/ppermute | solution.py:17
  1318.6 248.4 %reduce-scatter.11.cloned.1.call-start = ((), (), s32[]{:S(2)}) async-start(), calls=%async_computation.19 | async-start | bytes 4718592 | tf_op jit(solution)/shard_map/reduce_scatter | solution.py:354
  1323.5 335.7 %reduce-scatter.9.cloned.1.call-start = ((), (), s32[]{:S(2)}) async-start(), calls=%async_computation.18 | async-start | bytes 4718592 | tf_op jit(solution)/shard_map/reduce_scatter | solution.py:353
  1327.0 465.5 %reduce-scatter.19.cloned.1.call-start = ((), (), s32[]{:S(2)}) async-start(), calls=%async_computation.23 | async-start | bytes 7962624 | tf_op jit(solution)/shard_map/reduce_scatter | solution.py:358
  1334.6 590.7 %reduce-scatter.21.cloned.1.call-start = ((), (), s32[]{:S(2)}) async-start(), calls=%async_computation.24 | async-start | bytes 7962624 | tf_op jit(solution)/shard_map/reduce_scatter | solution.py:359
  1342.3 715.8 %reduce-scatter.23.cloned.1.call-start = ((), (), s32[]{:S(2)}) async-start(), calls=%async_computation.25 | async-start | bytes 7962624 | tf_op jit(solution)/shard_map/reduce_scatter | solution.py:360
  1350.1 840.9 %reduce-scatter.17.cloned.1.call-start = ((), (), s32[]{:S(2)}) async-start(), calls=%async_computation.22 | async-start | bytes 7962624 | tf_op jit(solution)/shard_map/reduce_scatter | solution.py:357
  1358.3 965.6 %reduce-scatter.13.cloned.1.call-start = ((), (), s32[]{:S(2)}) async-start(), calls=%async_computation.20 | async-start | bytes 7962624 | tf_op jit(solution)/shard_map/reduce_scatter | solution.py:355
  1364.4 1092.5 %reduce-scatter.15.cloned.1.call-start = ((), (), s32[]{:S(2)}) async-start(), calls=%async_computation.21 | async-start | bytes 7962624 | tf_op jit(solution)/shard_map/reduce_scatter | solution.py:356
  (77 other events, 2231.7 us)
Sparse Core Ops, SparseCore 0:
  10.1 51.9 all-gather.16
  64.2 47.6 all-gather.14
  113.9 65.6 all-gather.12
  181.6 92.4 all-gather.10
  276.0 88.9 all-gather.18
  580.0 87.2 all-reduce.7
  669.3 67.2 all-gather.20
  738.7 65.3 all-gather.22
  806.1 65.3 all-gather.24
  886.2 83.6 all-reduce.9
  1318.7 155.3 all-reduce.11
  1478.1 88.8 reduce-scatter.10
  1571.2 87.9 reduce-scatter.8
  1663.3 129.1 reduce-scatter.18
  1796.6 128.6 reduce-scatter.20
  1929.5 128.6 reduce-scatter.22
  2062.3 128.6 reduce-scatter.16
  2195.1 128.6 reduce-scatter.12
  2328.1 128.6 reduce-scatter.14
where the time goes:
time: 2470 us; the launch traced here: 2460 us
  waiting for transfers between devices  2050 us (83%)
  matrix products  132 us (5%)
  starting transfers between devices  85.1 us (3%)
  blocking collectives  80.6 us (3%)
  other arithmetic  62.5 us (3%)
  local copies, waits for them, and re-layouts  37.7 us (2%)
    ppermute x14, waiting for transfers between devices, passed_along(): return lax.ppermute(block, axis, route)  560 us
    reduce_scatter x1, waiting for transfers between devices, on_device(): lax.psum_scatter(glu_grad, 'seq', scatter_dimension=0, tiled=True)  133 us
    reduce_scatter x1, waiting for transfers between devices, on_device(): lax.psum_scatter(gate_grad, 'seq', scatter_dimension=0, tiled=True)  133 us
    reduce_scatter x1, waiting for transfers between devices, on_device(): lax.psum_scatter(value_grad, 'seq', scatter_dimension=0, tiled=True)  133 us
    reduce_scatter x1, waiting for transfers between devices, on_device(): lax.psum_scatter(down_grad, 'seq', scatter_dimension=1, tiled=True)  133 us
    reduce_scatter x1, waiting for transfers between devices, on_device(): lax.psum_scatter(out_grad, 'seq', scatter_dimension=1, tiled=True)  133 us
    reduce_scatter x1, waiting for transfers between devices, on_device(): lax.psum_scatter(up_grad, 'seq', scatter_dimension=0, tiled=True)  133 us
    psum x1, waiting for transfers between devices, on_device(): lax.psum(jnp.dot(hidden, full_down, preferred_element_type=jnp.float32),...  101 us
  transfers between devices with their start and end apart: 33, of which 31 were waited for; matrix products, arithmetic and copies ran while one was open for 5% of the time, Pallas kernels for 0%

commit v1 on v0

--- a/solution.py
+++ b/solution.py
@@ -248,7 +248,9 @@
     gate_act, gate_slope = swish_parts(gate_lin)
     group_flat = group_normed.reshape(row_count, local_heads * VAL)
     mixed = (gate_act * group_flat).astype(jnp.bfloat16)
-    attn_out = lax.psum(jnp.dot(mixed, full_out, preferred_element_type=jnp.float32), "tp")
+    attn_out = jnp.sum(
+        lax.all_gather(jnp.dot(mixed, full_out, preferred_element_type=jnp.float32), "tp"), axis=0
+    )
     middle = residual + attn_out
     normed_two, inv_two = normalize(middle, EPS_LAYER)
     ffn_in = (normed_two * full_ffn_gain.astype(jnp.float32)).astype(jnp.bfloat16)

time: 2470 us -> 2540 us (1.028)
  other arithmetic: 62.5 us -> 102 us
    all_gather x0 -> x1, waiting for transfers between devices: none -> 86 us  [on_device(): lax.all_gather(jnp.dot(mixed, full_out, preferred_element_type=jnp.float3...]
    psum x1 -> x0, waiting for transfers between devices: 65.3 us -> none  [on_device(): lax.psum(jnp.dot(mixed, full_out, preferred_element_type=jnp.float32), 'tp')]
  transfers between devices with their start and end apart: 33 -> 33, of which waited for: 31 -> 31; matrix products, arithmetic and copies ran while one was open for 5% -> 7% of each run, Pallas kernels for 0% -> 0%
where the time goes in v1:
time: 2540 us; the launch traced here: 2530 us
  waiting for transfers between devices  2040 us (80%)
  matrix products  146 us (6%)
  other arithmetic  102 us (4%)
  starting transfers between devices  101 us (4%)
  blocking collectives  85.2 us (3%)
  local copies, waits for them, and re-layouts  40.8 us (2%)
    ppermute x14, waiting for transfers between devices, passed_along(): return lax.ppermute(block, axis, route)  542 us
    reduce_scatter x1, waiting for transfers between devices, on_device(): lax.psum_scatter(glu_grad, 'seq', scatter_dimension=0, tiled=True)  133 us
    reduce_scatter x1, waiting for transfers between devices, on_device(): lax.psum_scatter(gate_grad, 'seq', scatter_dimension=0, tiled=True)  133 us
    reduce_scatter x1, waiting for transfers between devices, on_device(): lax.psum_scatter(down_grad, 'seq', scatter_dimension=1, tiled=True)  133 us
    reduce_scatter x1, waiting for transfers between devices, on_device(): lax.psum_scatter(value_grad, 'seq', scatter_dimension=0, tiled=True)  133 us
    reduce_scatter x1, waiting for transfers between devices, on_device(): lax.psum_scatter(out_grad, 'seq', scatter_dimension=1, tiled=True)  133 us
    reduce_scatter x1, waiting for transfers between devices, on_device(): lax.psum_scatter(up_grad, 'seq', scatter_dimension=0, tiled=True)  133 us
    ppermute x14, starting transfers between devices, passed_along(): return lax.ppermute(block, axis, route)  99.3 us
  transfers between devices with their start and end apart: 33, of which 31 were waited for; matrix products, arithmetic and copies ran while one was open for 7% of the time, Pallas kernels for 0%

profile of v1, /device:TPU:0, one launch (start us, length us, event | category | flops | bytes accessed | tf_op | source)
XLA Modules:
  0.0 2526.5 jit_solution(10184365343012352262)
XLA Ops:
  66.0 45.9 %all-gather.17.cloned.1.call-done = bf16[2048,512]{1,0:T(8,128)(2,1)} async-done(((bf16[256,512]{1,0:T(8,128)(2,1)}), bf16[2048,512]{1,0:T(8,128)(2,1)}) %all-gather.17.cloned.1.call-update) | async-done | bytes 2097168 | tf_op jit(solution)/shard_map/all_gather | solution.py:194
  124.1 55.5 %all-gather.15.cloned.1.call-done = bf16[2048,864]{0,1:T(8,128)(2,1)} async-done(((bf16[256,864]{0,1:T(8,128)(2,1)}), bf16[2048,864]{0,1:T(8,128)(2,1)}) %all-gather.15.cloned.1.call-update) | async-done | bytes 3538960 | tf_op jit(solution)/shard_map/all_gather | solution.py:196
  189.6 384.0 %while.20 = (s32[]{:T(128)}, f32[2,2,256,432]{2,3,1,0:T(8,128)}, f32[2]{0:T(128)S(1)}, f32[2,2,256,432]{2,3,1,0:T(8,128)}, s32[]{:T(128)}) while((s32[]{:T(128)}, f32[2,2,256,432]{2,3,1,0:T(8,128)}, f32[2]{0:T(128)S(1)}, f32[2,2,256,432]{2,3,1,0:T(8,128)}, s32[]{:T(128)}) %tuple.66), condition=%wide.region_3.4_spmd, body=%wide.region_2.3_spmd.sunk | while | flops 884738 | bytes 12386413 | solution.py:164
  197.7 53.6 %collective-permute-done = f32[2,2,256,432]{2,3,1,0:T(8,128)} collective-permute-done((f32[2,2,256,432]{2,3,1,0:T(8,128)}, f32[2,2,256,432]{2,3,1,0:T(8,128)}, u32[]{:S(2)}, u32[]{:S(2)}) %collective-permute-start) | collective-permute-done | bytes 1769504 | tf_op jit(solution)/shard_map/while/body/eval_jaxpr/ppermute | solution.py:17
  273.4 41.2 %collective-permute-done = f32[2,2,256,432]{2,3,1,0:T(8,128)} collective-permute-done((f32[2,2,256,432]{2,3,1,0:T(8,128)}, f32[2,2,256,432]{2,3,1,0:T(8,128)}, u32[]{:S(2)}, u32[]{:S(2)}) %collective-permute-start) | collective-permute-done | bytes 1769504 | tf_op jit(solution)/shard_map/while/body/eval_jaxpr/ppermute | solution.py:17
  622.1 86.0 %all-gather.29.cloned.1.call-done = f32[2048,2048]{1,0:T(8,128)} async-done(((f32[512,2048]{1,0:T(8,128)}), f32[2048,2048]{1,0:T(8,128)}) %all-gather.29.cloned.1.call-update) | async-done | bytes 16777232 | tf_op jit(solution)/shard_map/all_gather | solution.py:252
  724.9 52.4 %all-gather.23.cloned.1.call-done = bf16[2048,864]{0,1:T(8,128)(2,1)} async-done(((bf16[256,864]{0,1:T(8,128)(2,1)}), bf16[2048,864]{0,1:T(8,128)(2,1)}) %all-gather.23.cloned.1.call-update) | async-done | bytes 3538960 | tf_op jit(solution)/shard_map/all_gather | solution.py:199
  783.2 61.5 %all-gather.25.cloned.1.call-done = bf16[2048,864]{0,1:T(8,128)(2,1)} async-done(((bf16[256,864]{0,1:T(8,128)(2,1)}), bf16[2048,864]{0,1:T(8,128)(2,1)}) %all-gather.25.cloned.1.call-update) | async-done | bytes 3538960 | tf_op jit(solution)/shard_map/all_gather | solution.py:200
  850.6 61.5 %all-gather.27.cloned.1.call-done = bf16[864,2048]{1,0:T(8,128)(2,1)} async-done(((bf16[864,256]{1,0:T(8,128)(2,1)}), bf16[864,2048]{1,0:T(8,128)(2,1)}) %all-gather.27.cloned.1.call-update) | async-done | bytes 3538960 | tf_op jit(solution)/shard_map/all_gather | solution.py:201
  933.6 77.2 %all-reduce.7.cloned.1.call-done = f32[512,2048]{1,0:T(8,128)} async-done(((f32[512,2048]{1,0:T(8,128)}), f32[512,2048]{1,0:T(8,128)}) %all-reduce.7.cloned.1.call-update) | async-done | bytes 4194320 | tf_op jit(solution)/shard_map/psum | solution.py:295
  1046.9 307.6 %while.21 = (s32[]{:T(128)}, f32[2,2,256,432]{2,3,1,0:T(8,128)}, f32[2]{0:T(128)S(1)}, f32[2,2,256,432]{2,3,1,0:T(8,128)}, s32[]{:T(128)}) while((s32[]{:T(128)}, f32[2,2,256,432]{2,3,1,0:T(8,128)}, f32[2]{0:T(128)S(1)}, f32[2,2,256,432]{2,3,1,0:T(8,128)}, s32[]{:T(128)}) %tuple.111), condition=%wide.region_16.17_spmd, body=%wide.region_15.16_spmd.sunk | while | flops 884738 | bytes 12386413 | solution.py:172
  1051.7 40.9 %collective-permute-done.1 = f32[2,2,256,432]{2,3,1,0:T(8,128)} collective-permute-done((f32[2,2,256,432]{2,3,1,0:T(8,128)}, f32[2,2,256,432]{2,3,1,0:T(8,128)}, u32[]{:S(2)}, u32[]{:S(2)}) %collective-permute-start.1) | collective-permute-done | bytes 1769504 | tf_op jit(solution)/shard_map/while/body/eval_jaxpr/ppermute | solution.py:17
  1097.4 40.7 %collective-permute-done.1 = f32[2,2,256,432]{2,3,1,0:T(8,128)} collective-permute-done((f32[2,2,256,432]{2,3,1,0:T(8,128)}, f32[2,2,256,432]{2,3,1,0:T(8,128)}, u32[]{:S(2)}, u32[]{:S(2)}) %collective-permute-start.1) | collective-permute-done | bytes 1769504 | tf_op jit(solution)/shard_map/while/body/eval_jaxpr/ppermute | solution.py:17
  1143.0 40.1 %collective-permute-done.1 = f32[2,2,256,432]{2,3,1,0:T(8,128)} collective-permute-done((f32[2,2,256,432]{2,3,1,0:T(8,128)}, f32[2,2,256,432]{2,3,1,0:T(8,128)}, u32[]{:S(2)}, u32[]{:S(2)}) %collective-permute-start.1) | collective-permute-done | bytes 1769504 | tf_op jit(solution)/shard_map/while/body/eval_jaxpr/ppermute | solution.py:17
  1187.9 39.3 %collective-permute-done.1 = f32[2,2,256,432]{2,3,1,0:T(8,128)} collective-permute-done((f32[2,2,256,432]{2,3,1,0:T(8,128)}, f32[2,2,256,432]{2,3,1,0:T(8,128)}, u32[]{:S(2)}, u32[]{:S(2)}) %collective-permute-start.1) | collective-permute-done | bytes 1769504 | tf_op jit(solution)/shard_map/while/body/eval_jaxpr/ppermute | solution.py:17
  1441.0 95.9 %all-reduce.9.cloned.1.call-done = (f32[512,2048]{1,0:T(8,128)}, f32[512,2048]{1,0:T(8,128)}) async-done(((f32[512,2048]{1,0:T(8,128)}, f32[512,2048]{1,0:T(8,128)}), (f32[512,2048]{1,0:T(8,128)}, f32[512,2048]{1,0:T(8,128)})) %all-reduce.9.cloned.1.call-update) | async-done | bytes 8388624 | tf_op jit(solution)/shard_map/psum | solution.py:261
  1590.0 39.9 %reduce-scatter.11.cloned.1.call-done = f32[256,512]{1,0:T(8,128)} async-done(((f32[2048,512]{1,0:T(8,128)}), f32[256,512]{1,0:T(8,128)}) %reduce-scatter.11.cloned.1.call-update) | async-done | bytes 524304 | tf_op jit(solution)/shard_map/reduce_scatter | solution.py:356
  1629.9 92.2 %reduce-scatter.9.cloned.1.call-done = f32[256,512]{1,0:T(8,128)} async-done(((f32[2048,512]{1,0:T(8,128)}), f32[256,512]{1,0:T(8,128)}) %reduce-scatter.9.cloned.1.call-update) | async-done | bytes 524304 | tf_op jit(solution)/shard_map/reduce_scatter | solution.py:355
  1722.1 133.3 %reduce-scatter.19.cloned.1.call-done = f32[256,864]{0,1:T(8,128)} async-done(((f32[2048,864]{0,1:T(8,128)}), f32[256,864]{0,1:T(8,128)}) %reduce-scatter.19.cloned.1.call-update) | async-done | bytes 884752 | tf_op jit(solution)/shard_map/reduce_scatter | solution.py:360
  1855.4 132.8 %reduce-scatter.21.cloned.1.call-done = f32[256,864]{0,1:T(8,128)} async-done(((f32[2048,864]{0,1:T(8,128)}), f32[256,864]{0,1:T(8,128)}) %reduce-scatter.21.cloned.1.call-update) | async-done | bytes 884752 | tf_op jit(solution)/shard_map/reduce_scatter | solution.py:361
  1988.2 132.8 %reduce-scatter.23.cloned.1.call-done = f32[864,256]{1,0:T(8,128)} async-done(((f32[864,2048]{1,0:T(8,128)}), f32[864,256]{1,0:T(8,128)}) %reduce-scatter.23.cloned.1.call-update) | async-done | bytes 884752 | tf_op jit(solution)/shard_map/reduce_scatter | solution.py:362
  2121.0 132.8 %reduce-scatter.17.cloned.1.call-done = f32[864,256]{1,0:T(8,128)} async-done(((f32[864,2048]{1,0:T(8,128)}), f32[864,256]{1,0:T(8,128)}) %reduce-scatter.17.cloned.1.call-update) | async-done | bytes 884752 | tf_op jit(solution)/shard_map/reduce_scatter | solution.py:359
  2253.8 132.8 %reduce-scatter.13.cloned.1.call-done = f32[256,864]{0,1:T(8,128)} async-done(((f32[2048,864]{0,1:T(8,128)}), f32[256,864]{0,1:T(8,128)}) %reduce-scatter.13.cloned.1.call-update) | async-done | bytes 884752 | tf_op jit(solution)/shard_map/reduce_scatter | solution.py:357
  2386.6 133.0 %reduce-scatter.15.cloned.1.call-done = f32[256,864]{0,1:T(8,128)} async-done(((f32[2048,864]{0,1:T(8,128)}), f32[256,864]{0,1:T(8,128)}) %reduce-scatter.15.cloned.1.call-update) | async-done | bytes 884752 | tf_op jit(solution)/shard_map/reduce_scatter | solution.py:358
  (285 shorter events, 788.6 us)
Async XLA Ops:
  7.2 54.9 %all-gather.19.cloned.1.call-start = ((), (), s32[]{:S(2)}) async-start(), calls=%async_computation.11 | async-start | bytes 2359296 | tf_op jit(solution)/shard_map/all_gather | solution.py:195
  7.9 103.9 %all-gather.17.cloned.1.call-start = ((), (), s32[]{:S(2)}) async-start(), calls=%async_computation.10 | async-start | bytes 2359296 | tf_op jit(solution)/shard_map/all_gather | solution.py:194
  8.7 171.0 %all-gather.15.cloned.1.call-start = ((), (), s32[]{:S(2)}) async-start(), calls=%async_computation.9 | async-start | bytes 3981312 | tf_op jit(solution)/shard_map/all_gather | solution.py:196
  9.4 572.5 %all-gather.13.cloned.1.call-start = ((), (), s32[]{:S(2)}) async-start(), calls=%async_computation.8 | async-start | bytes 3981312 | tf_op jit(solution)/shard_map/all_gather | solution.py:197
  10.0 578.7 %all-gather.21.cloned.1.call-start = ((), (), s32[]{:S(2)}) async-start(), calls=%async_computation.12 | async-start | bytes 3981312 | tf_op jit(solution)/shard_map/all_gather | solution.py:198
  10.6 697.5 %all-gather.29.cloned.1.call-start = ((), (), s32[]{:S(2)}) async-start(), calls=%async_computation.25 | async-start | bytes 20971520 | tf_op jit(solution)/shard_map/all_gather | solution.py:252
  193.1 58.2 %collective-permute-start = (f32[2,2,256,432]{2,3,1,0:T(8,128)}, f32[2,2,256,432]{2,3,1,0:T(8,128)}, u32[]{:S(2)}, u32[]{:S(2)}) collective-permute-start(f32[2,2,256,432]{2,3,1,0:T(8,128)} %multiply_add_fusion.5), channel_id=1, source_target_pairs={{0,4},{4,8},{8,12},{12,16},{16,20},{20,24},{24,28},{1,5},{5,9},{9,... | collective-permute-start | bytes 5308424 | tf_op jit(solution)/shard_map/while/body/eval_jaxpr/ppermute | solution.py:17
  254.9 59.7 %collective-permute-start = (f32[2,2,256,432]{2,3,1,0:T(8,128)}, f32[2,2,256,432]{2,3,1,0:T(8,128)}, u32[]{:S(2)}, u32[]{:S(2)}) collective-permute-start(f32[2,2,256,432]{2,3,1,0:T(8,128)} %multiply_add_fusion.5), channel_id=1, source_target_pairs={{0,4},{4,8},{8,12},{12,16},{16,20},{20,24},{24,28},{1,5},{5,9},{9,... | collective-permute-start | bytes 5308424 | tf_op jit(solution)/shard_map/while/body/eval_jaxpr/ppermute | solution.py:17
  318.1 58.8 %collective-permute-start = (f32[2,2,256,432]{2,3,1,0:T(8,128)}, f32[2,2,256,432]{2,3,1,0:T(8,128)}, u32[]{:S(2)}, u32[]{:S(2)}) collective-permute-start(f32[2,2,256,432]{2,3,1,0:T(8,128)} %multiply_add_fusion.5), channel_id=1, source_target_pairs={{0,4},{4,8},{8,12},{12,16},{16,20},{20,24},{24,28},{1,5},{5,9},{9,... | collective-permute-start | bytes 5308424 | tf_op jit(solution)/shard_map/while/body/eval_jaxpr/ppermute | solution.py:17
  380.4 55.4 %collective-permute-start = (f32[2,2,256,432]{2,3,1,0:T(8,128)}, f32[2,2,256,432]{2,3,1,0:T(8,128)}, u32[]{:S(2)}, u32[]{:S(2)}) collective-permute-start(f32[2,2,256,432]{2,3,1,0:T(8,128)} %multiply_add_fusion.5), channel_id=1, source_target_pairs={{0,4},{4,8},{8,12},{12,16},{16,20},{20,24},{24,28},{1,5},{5,9},{9,... | collective-permute-start | bytes 5308424 | tf_op jit(solution)/shard_map/while/body/eval_jaxpr/ppermute | solution.py:17
  483.8 45.6 %collective-permute-start = (f32[2,2,256,432]{2,3,1,0:T(8,128)}, f32[2,2,256,432]{2,3,1,0:T(8,128)}, u32[]{:S(2)}, u32[]{:S(2)}) collective-permute-start(f32[2,2,256,432]{2,3,1,0:T(8,128)} %multiply_add_fusion.5), channel_id=1, source_target_pairs={{0,4},{4,8},{8,12},{12,16},{16,20},{20,24},{24,28},{1,5},{5,9},{9,... | collective-permute-start | bytes 5308424 | tf_op jit(solution)/shard_map/while/body/eval_jaxpr/ppermute | solution.py:17
  595.4 181.9 %all-gather.23.cloned.1.call-start = ((), (), s32[]{:S(2)}) async-start(), calls=%async_computation.13 | async-start | bytes 3981312 | tf_op jit(solution)/shard_map/all_gather | solution.py:199
  596.2 248.5 %all-gather.25.cloned.1.call-start = ((), (), s32[]{:S(2)}) async-start(), calls=%async_computation.14 | async-start | bytes 3981312 | tf_op jit(solution)/shard_map/all_gather | solution.py:200
  596.9 315.2 %all-gather.27.cloned.1.call-start = ((), (), s32[]{:S(2)}) async-start(), calls=%async_computation.15 | async-start | bytes 3981312 | tf_op jit(solution)/shard_map/all_gather | solution.py:201
  597.7 413.1 %all-reduce.7.cloned.1.call-start = ((), (), s32[]{:S(2)}) async-start(), calls=%async_computation.16 | async-start | bytes 8388608 | tf_op jit(solution)/shard_map/psum | solution.py:295
  926.9 610.0 %all-reduce.9.cloned.1.call-start = ((), (), s32[]{:S(2)}) async-start(), calls=%async_computation.26 | async-start | bytes 16777216 | tf_op jit(solution)/shard_map/psum | solution.py:261
  1381.4 248.4 %reduce-scatter.11.cloned.1.call-start = ((), (), s32[]{:S(2)}) async-start(), calls=%async_computation.18 | async-start | bytes 4718592 | tf_op jit(solution)/shard_map/reduce_scatter | solution.py:356
  1387.3 334.7 %reduce-scatter.9.cloned.1.call-start = ((), (), s32[]{:S(2)}) async-start(), calls=%async_computation.17 | async-start | bytes 4718592 | tf_op jit(solution)/shard_map/reduce_scatter | solution.py:355
  1392.4 463.0 %reduce-scatter.19.cloned.1.call-start = ((), (), s32[]{:S(2)}) async-start(), calls=%async_computation.22 | async-start | bytes 7962624 | tf_op jit(solution)/shard_map/reduce_scatter | solution.py:360
  1400.0 588.2 %reduce-scatter.21.cloned.1.call-start = ((), (), s32[]{:S(2)}) async-start(), calls=%async_computation.23 | async-start | bytes 7962624 | tf_op jit(solution)/shard_map/reduce_scatter | solution.py:361
  1407.7 713.3 %reduce-scatter.23.cloned.1.call-start = ((), (), s32[]{:S(2)}) async-start(), calls=%async_computation.24 | async-start | bytes 7962624 | tf_op jit(solution)/shard_map/reduce_scatter | solution.py:362
  1415.4 838.4 %reduce-scatter.17.cloned.1.call-start = ((), (), s32[]{:S(2)}) async-start(), calls=%async_computation.21 | async-start | bytes 7962624 | tf_op jit(solution)/shard_map/reduce_scatter | solution.py:359
  1423.8 962.8 %reduce-scatter.13.cloned.1.call-start = ((), (), s32[]{:S(2)}) async-start(), calls=%async_computation.19 | async-start | bytes 7962624 | tf_op jit(solution)/shard_map/reduce_scatter | solution.py:357
  1431.5 1088.1 %reduce-scatter.15.cloned.1.call-start = ((), (), s32[]{:S(2)}) async-start(), calls=%async_computation.20 | async-start | bytes 7962624 | tf_op jit(solution)/shard_map/reduce_scatter | solution.py:358
  (59 other events, 976.6 us)
Sparse Core Ops, SparseCore 0:
  10.1 51.9 all-gather.18
  64.2 47.6 all-gather.16
  113.9 65.6 all-gather.14
  181.5 89.0 all-gather.12
  272.5 91.7 all-gather.20
  595.5 112.4 all-gather.28
  710.1 67.1 all-gather.22
  779.3 65.3 all-gather.24
  846.8 65.3 all-gather.26
  927.0 83.6 all-reduce.6
  1381.6 155.2 all-reduce.8
  1541.0 88.8 reduce-scatter.10
  1634.1 87.9 reduce-scatter.8
  1726.2 129.1 reduce-scatter.18
  1859.5 128.6 reduce-scatter.20
  1992.3 128.6 reduce-scatter.22
  2125.1 128.6 reduce-scatter.16
  2257.9 128.6 reduce-scatter.12
  2390.9 128.6 reduce-scatter.14
